TPU v7x, 32 devices: a whole 2x2x4 slice. The times are simulated.
32 devices in a mesh: pair: 8 (over y, x, core), aux: 4 (over z).
Axes of the slice: x: 2, y: 2, z: 4, core: 2. Of those that a mesh axis runs over, the one named last changes fastest.
Arguments:
- integrals: bfloat16 [512, 256, 64], P(('pair', 'aux')), may hold values from -6 to 6
- amplitudes: bfloat16 [512, 64, 64], P(('pair', 'aux')), may hold values from -0.75 to 0.75
- pno_density: bfloat16 [512, 64, 64], P(('pair', 'aux')), may hold values from -6 to 6
- pno_coef: bfloat16 [512, 256, 64], P(('pair', 'aux')), may hold values from -0.75 to 0.75
- pao_blocks: int32 [512, 2], P(('pair', 'aux')), may hold values from 0 to 5, all different within a row
- aux_slice: int32 [512, 2], P(('pair', 'aux')), may hold values from 0 to 3, all different within a row; in each aligned block of 16 rows (0 to 15, 16 to 31, ...) at most 16 rows name the same one
- aux_offset: int32 [512, 2], P(('pair', 'aux')), may hold values from 0 to 3
Outputs:
- aux_density: float32 [2048, 768], P('aux', 'pair')
- virtual_density: float32 [768, 768], P('aux', 'pair')
Inputs may be any that keep to these rules, and one draw needn't show every extreme that they name: `pao_blocks`: the 2 blocks of a pair are different. `aux_slice`: the 2 slices of a pair are different; among the pairs of one device no slice is named more than 16 times, and in every draw some device names some slice exactly 16 times.
All inputs are finite; a program needn't handle non-finite values.
Results may differ from a plain program's by a relative error of at most 0.0041.
Values may be sent and summed in bfloat16 or wider, within the bound.
A program may use at most 64 MiB of HBM per device.

v0:
```python
import math

import jax
import jax.numpy as jnp
from jax import lax
from jax.sharding import PartitionSpec as P

NBLK = 6
ABPO = 4


def on_device(integrals, amplitudes, pno_density, pno_coef, pao_blocks, aux_slice, aux_offset):
    n_pair = lax.axis_size("pair")
    n_aux = lax.axis_size("aux")
    pair_count, domain_rows, pno_rank = pno_coef.shape
    aux_dom = aux_slice.shape[1]
    pao_dom = pao_blocks.shape[1]
    pao_block = domain_rows // pao_dom
    aux_block = integrals.shape[1] // aux_dom
    ao_count = NBLK * pao_block
    capacity = max(2, 2 * pair_count * aux_dom // n_aux)
    out_scale = 1.0 / math.sqrt(pair_count * n_pair)
    slot_count = pair_count * aux_dom
    three_index = jnp.einsum(
        "pqr,prs->pqs", integrals, amplitudes, preferred_element_type=jnp.float32
    ).astype(jnp.bfloat16)
    owners = aux_slice.reshape(slot_count)
    owner_hot = (owners[:, None] == jnp.arange(n_aux, dtype=jnp.int32)[None, :]).astype(jnp.int32)
    before = jnp.cumsum(owner_hot, 0) - owner_hot
    slot_rank = jnp.sum(before * owner_hot, 1)
    target = owners * capacity + slot_rank
    routing = jnp.arange(n_aux * capacity, dtype=jnp.int32)[:, None] == target[None, :]
    labels = (
        jnp.concatenate(
            [aux_offset.reshape(slot_count, 1), jnp.repeat(pao_blocks, aux_dom, axis=0)], 1
        )
        + 1
    )
    label_buffer = (jnp.dot(routing.astype(jnp.int32), labels) - 1).reshape(
        n_aux, capacity, 1 + pao_dom
    )
    routing_bf = routing.astype(jnp.bfloat16)
    index_flat = three_index.reshape(slot_count, aux_block * pno_rank)
    index_buffer = jnp.dot(routing_bf, index_flat, preferred_element_type=jnp.float32).astype(
        jnp.bfloat16
    )
    index_buffer = index_buffer.reshape(n_aux, capacity, aux_block, pno_rank)
    pair_routing = (
        routing.reshape(n_aux * capacity, pair_count, aux_dom).sum(-1).astype(jnp.bfloat16)
    )
    coef_flat = pno_coef.reshape(pair_count, domain_rows * pno_rank)
    coef_buffer = jnp.dot(pair_routing, coef_flat, preferred_element_type=jnp.float32).astype(
        jnp.bfloat16
    )
    coef_buffer = coef_buffer.reshape(n_aux, capacity, domain_rows, pno_rank)
    index_part = lax.all_to_all(index_buffer, "aux", split_axis=0, concat_axis=0, tiled=True)
    coef_part = lax.all_to_all(coef_buffer, "aux", split_axis=0, concat_axis=0, tiled=True)
    label_part = lax.all_to_all(label_buffer, "aux", split_axis=0, concat_axis=0, tiled=True)
    back = jnp.einsum(
        "ncxr,ncyr->ncxy", index_part, coef_part, preferred_element_type=jnp.float32
    ).astype(jnp.bfloat16)
    got_labels = label_part
    received_count = n_aux * capacity
    pieces = back.reshape(received_count, aux_block, pao_dom, pao_block)
    got_labels = got_labels.reshape(received_count, 1 + pao_dom)
    offset_hot = got_labels[:, 0:1] == jnp.arange(ABPO, dtype=jnp.int32)[None, :]
    column_hot = got_labels[:, 1:, None] == jnp.arange(NBLK, dtype=jnp.int32)[None, None, :]
    placement = (offset_hot[:, None, :, None] & column_hot[:, :, None, :]).astype(jnp.bfloat16)
    gamma_part = jnp.einsum(
        "sxhy,shok->oxky", pieces, placement, preferred_element_type=jnp.float32
    )
    gamma_part = gamma_part.reshape(ABPO * aux_block, ao_count)
    aux_density = lax.psum_scatter(gamma_part, "pair", scatter_dimension=1, tiled=True) * out_scale
    weighted = jnp.einsum(
        "pyr,prs->pys", pno_coef, pno_density, preferred_element_type=jnp.float32
    ).astype(jnp.bfloat16)
    block_hot = (pao_blocks[:, :, None] == jnp.arange(NBLK, dtype=jnp.int32)[None, None, :]).astype(
        jnp.bfloat16
    )
    weighted_rows = jnp.einsum(
        "pak,paxr->kxpr",
        block_hot,
        weighted.reshape(pair_count, pao_dom, pao_block, pno_rank),
        preferred_element_type=jnp.float32,
    ).astype(jnp.bfloat16)
    weighted_rows = weighted_rows.reshape(ao_count, pair_count * pno_rank)
    coef_rows = jnp.einsum(
        "pak,paxr->kxpr",
        block_hot,
        pno_coef.reshape(pair_count, pao_dom, pao_block, pno_rank),
        preferred_element_type=jnp.float32,
    ).astype(jnp.bfloat16)
    coef_rows = coef_rows.reshape(ao_count, pair_count * pno_rank)
    virt_part = lax.dot_general(
        weighted_rows, coef_rows, (((1,), (1,)), ((), ())), preferred_element_type=jnp.float32
    )
    row_owned = lax.psum_scatter(virt_part, "aux", scatter_dimension=0, tiled=True)
    virtual_density = lax.psum_scatter(row_owned, "pair", scatter_dimension=1, tiled=True)
    return (aux_density, virtual_density * out_scale)


def solution(mesh):
    in_specs = (
        P(("pair", "aux"), None, None),
        P(("pair", "aux"), None, None),
        P(("pair", "aux"), None, None),
        P(("pair", "aux"), None, None),
        P(("pair", "aux"), None),
        P(("pair", "aux"), None),
        P(("pair", "aux"), None),
    )
    out_specs = (P("aux", "pair"), P("aux", "pair"))
    return jax.shard_map(
        on_device, mesh=mesh, in_specs=in_specs, out_specs=out_specs, check_vma=False
    )
```

profile of v0, /device:TPU:0, one launch (start us, length us, event | category | flops | bytes accessed | tf_op | source)
XLA Modules:
  0.0 246.8 jit_solution(5332857708423388799)
XLA Ops:
  7.2 0.8 copy.78
  8.0 0.1 reshape.94
  8.2 0.2 select_reduce_fusion
  8.4 0.8 broadcast_in_dim.2
  9.2 0.1 reshape.96
  9.3 0.8 copy.79
  10.0 0.1 reshape.95
  10.1 0.1 convolution_add_fusion
  10.2 0.1 reshape.97
  10.3 0.6 copy.80
  11.0 6.3 %all-to-all-start = ((s32[4,16,3]{1,2,0:T(4,128)}), s32[4,16,3]{1,2,0:T(4,128)S(1)}, u32[]{:S(2)}, u32[]{:S(2)}) async-start(s32[4,16,3]{1,2,0:T(4,128)} %copy.80), calls=%async_computation | async-start | bytes 16384 | tf_op jit(solution)/shard_map/all_to_all | solution.py:58
  17.3 1.3 convolution_convert_fusion.6
  18.6 0.5 copy.83
  19.1 0.8 reshape.99
  20.0 1.4 convolution_convert_fusion.1
  21.4 1.1 convolution_convert_fusion.5
  22.5 0.1 copy.91
  22.6 3.3 %reshape.100 = bf16[4,16,128,64]{3,2,1,0:T(8,128)(2,1)S(1)} reshape(bf16[64,8192]{1,0:T(8,128)(2,1)} %convolution_convert_fusion.1) | data formatting | bytes 2097152 | tf_op jit(solution)/shard_map/reshape | solution.py:47
  25.8 1.7 copy.84
  27.5 2.0 reshape.105
  29.5 5.1 %all-to-all-start.1 = ((bf16[4,16,128,64]{2,3,1,0:T(8,128)(2,1)}), bf16[4,16,128,64]{2,3,1,0:T(8,128)(2,1)}, u32[]{:S(2)}, u32[]{:S(2)}) async-start(bf16[4,16,128,64]{2,3,1,0:T(8,128)(2,1)} %copy.84), calls=%async_computation.1 | async-start | bytes 2097152 | tf_op jit(solution)/shard_map/all_to_all | solution.py:56
  34.6 1.9 convolution_convert_fusion.4
  36.4 0.9 reshape.107
  37.4 2.0 convolution_convert_fusion.3
  39.3 3.0 %fusion.3 = f32[768,768]{1,0:T(8,128)} fusion(bf16[128,8,6,128]{3,2,1,0:T(8,128)(2,1)S(1)} %bitcast.70, bf16[128,8,6,128]{3,2,1,0:T(8,128)(2,1)S(1)} %bitcast.69), kind=kOutput, calls=%fused_computation.8 | convolution fusion | flops 1207959552 | bytes 5505024 | tf_op jit(solution)/shard_map/dot_general | solution.py:94
  42.3 0.1 reduce_sum.21
  42.4 0.5 copy.86
  42.9 0.1 copy.85
  43.0 0.8 reshape.101
  43.8 0.1 convert_reduce_fusion
  43.9 0.7 convolution_convert_fusion
  44.6 5.5 %reshape.102 = bf16[4,16,256,64]{3,2,1,0:T(8,128)(2,1)} reshape(bf16[64,16384]{1,0:T(8,128)(2,1)S(1)} %convolution_convert_fusion) | data formatting | bytes 4194304 | tf_op jit(solution)/shard_map/reshape | solution.py:55
  50.2 4.8 %copy.87 = bf16[4,16,256,64]{2,3,1,0:T(8,128)(2,1)} copy(bf16[4,16,256,64]{3,2,1,0:T(8,128)(2,1)} %reshape.102) | data formatting | bytes 4194304 | tf_op jit(solution)/shard_map/reshape | solution.py:55
  55.0 21.5 %all-to-all-done.1 = bf16[4,16,128,64]{2,3,1,0:T(8,128)(2,1)} async-done(((bf16[4,16,128,64]{2,3,1,0:T(8,128)(2,1)}), bf16[4,16,128,64]{2,3,1,0:T(8,128)(2,1)}, u32[]{:S(2)}, u32[]{:S(2)}) %all-to-all-start.1) | async-done | bytes 1048608 | tf_op jit(solution)/shard_map/all_to_all | solution.py:56
  76.5 6.6 %all-to-all-start.2 = ((bf16[4,16,256,64]{2,3,1,0:T(8,128)(2,1)}), bf16[4,16,256,64]{2,3,1,0:T(8,128)(2,1)S(1)}, u32[]{:S(2)}, u32[]{:S(2)}) async-start(bf16[4,16,256,64]{2,3,1,0:T(8,128)(2,1)} %copy.87), calls=%async_computation.2 | async-start | bytes 4194304 | tf_op jit(solution)/shard_map/all_to_all | solution.py:57
  83.1 0.1 reshape.98
  83.2 59.4 %all-to-all-done.2 = bf16[4,16,256,64]{2,3,1,0:T(8,128)(2,1)S(1)} async-done(((bf16[4,16,256,64]{2,3,1,0:T(8,128)(2,1)}), bf16[4,16,256,64]{2,3,1,0:T(8,128)(2,1)S(1)}, u32[]{:S(2)}, u32[]{:S(2)}) %all-to-all-start.2) | async-done | bytes 2097184 | tf_op jit(solution)/shard_map/all_to_all | solution.py:57
  142.6 4.5 %convolution_convert_fusion.2 = bf16[4,16,128,256]{3,2,1,0:T(8,128)(2,1)} fusion(bf16[4,16,128,64]{2,3,1,0:T(8,128)(2,1)} %all-to-all-done.1, bf16[4,16,256,64]{2,3,1,0:T(8,128)(2,1)S(1)} %all-to-all-done.2), kind=kOutput, calls=%fused_computation.5 | convolution fusion | flops 270532608 | bytes 7340032 | tf_op jit(solution)/shard_map/ncxr,ncyr->ncxy/dot_general | solution.py:59
  147.0 7.0 %reshape.103 = bf16[64,128,2,128]{3,2,1,0:T(2,128)(2,1)} reshape(bf16[4,16,128,256]{3,2,1,0:T(8,128)(2,1)} %convolution_convert_fusion.2) | data formatting | bytes 8388608 | tf_op jit(solution)/shard_map/reshape | solution.py:64
  154.0 6.9 %fusion = f32[4,6,128,128,1]{3,1,4,2,0:T(8,128)S(1)} fusion(bf16[64,128,2,128]{3,2,1,0:T(2,128)(2,1)} %reshape.103, pred[64,2,6]{0,2,1:T(8,128)(4,1)S(1)} %iota_compare_fusion.8, pred[64,4]{0,1:T(4,128)(4,1)S(1)} %iota_compare_fusion.9), kind=kOutput, calls=%fused_computation.2 | convolution fusion | flops 100666368 | bytes 5768192 | tf_op jit(solution)/shard_map/sxhy,shok->oxky/dot_general | solution.py:69
  160.9 0.4 copy.116
  161.2 1.6 copy.97
  163.0 2.2 copy.98
  165.2 35.2 %reduce-scatter.6.cloned.1.call-done = f32[512,96]{0,1:T(8,128)} async-done(((f32[512,768]{0,1:T(8,128)}), f32[512,96]{0,1:T(8,128)}) %reduce-scatter.6.cloned.1.call-update) | async-done | bytes 196624 | tf_op jit(solution)/shard_map/reduce_scatter | solution.py:73
  200.5 1.6 broadcast_multiply_fusion
  202.1 36.5 %reduce-scatter.10.cloned.1.call-done = f32[96,192]{1,0:T(8,128)} async-done(((f32[768,192]{1,0:T(8,128)}), f32[96,192]{1,0:T(8,128)}) %reduce-scatter.10.cloned.1.call-update) | async-done | bytes 73744
  238.6 1.0 copy.99
  239.6 0.7 broadcast_multiply_fusion.1
  (27 shorter events, 0.3 us)
Async XLA Ops:
  7.2 10.1 %copy-start = (bf16[16,256,64]{1,2,0:T(8,128)(2,1)S(1)}, bf16[16,256,64]{1,2,0:T(8,128)(2,1)}, u32[]{:S(2)}) copy-start(bf16[16,256,64]{1,2,0:T(8,128)(2,1)} %param.7) | copy-start | bytes 1572868
  11.0 18.5 %all-to-all-start = ((s32[4,16,3]{1,2,0:T(4,128)}), s32[4,16,3]{1,2,0:T(4,128)S(1)}, u32[]{:S(2)}, u32[]{:S(2)}) async-start(s32[4,16,3]{1,2,0:T(4,128)} %copy.80), calls=%async_computation | async-start | bytes 16384 | tf_op jit(solution)/shard_map/all_to_all | solution.py:58
  18.6 2.7 %copy-start.1 = (bf16[16,256,64]{1,2,0:T(8,128)(2,1)S(1)}, bf16[16,256,64]{1,2,0:T(8,128)(2,1)}, u32[]{:S(2)}) copy-start(bf16[16,256,64]{1,2,0:T(8,128)(2,1)} %param.10) | copy-start | bytes 1572868
  18.6 2.7 %copy-start.2 = (bf16[16,64,64]{2,1,0:T(8,128)(2,1)S(1)}, bf16[16,64,64]{2,1,0:T(8,128)(2,1)}, u32[]{:S(2)}) copy-start(bf16[16,64,64]{2,1,0:T(8,128)(2,1)} %param.9) | copy-start | bytes 393220
  19.1 3.4 %copy-start.3 = (s32[16,2]{0,1:T(2,128)S(1)}, s32[16,2]{0,1:T(2,128)}, u32[]{:S(2)}) copy-start(s32[16,2]{0,1:T(2,128)} %param.11) | copy-start | bytes 388
  29.5 47.0 %all-to-all-start.1 = ((bf16[4,16,128,64]{2,3,1,0:T(8,128)(2,1)}), bf16[4,16,128,64]{2,3,1,0:T(8,128)(2,1)}, u32[]{:S(2)}, u32[]{:S(2)}) async-start(bf16[4,16,128,64]{2,3,1,0:T(8,128)(2,1)} %copy.84), calls=%async_computation.1 | async-start | bytes 2097152 | tf_op jit(solution)/shard_map/all_to_all | solution.py:56
  34.6 128.4 %reduce-scatter.8.cloned.1.call-start = ((), (), s32[]{:S(2)}) async-start(), calls=%async_computation.7 | async-start | bytes 2949120 | tf_op jit(solution)/shard_map/reduce_scatter | solution.py:97
  42.3 1.5 copy-start.4
  76.5 66.1 %all-to-all-start.2 = ((bf16[4,16,256,64]{2,3,1,0:T(8,128)(2,1)}), bf16[4,16,256,64]{2,3,1,0:T(8,128)(2,1)S(1)}, u32[]{:S(2)}, u32[]{:S(2)}) async-start(bf16[4,16,256,64]{2,3,1,0:T(8,128)(2,1)} %copy.87), calls=%async_computation.2 | async-start | bytes 4194304 | tf_op jit(solution)/shard_map/all_to_all | solution.py:57
  83.1 117.4 %reduce-scatter.6.cloned.1.call-start = ((), (), s32[]{:S(2)}) async-start(), calls=%async_computation.6 | async-start | bytes 1769472 | tf_op jit(solution)/shard_map/reduce_scatter | solution.py:73
  162.9 75.7 %reduce-scatter.10.cloned.1.call-start = ((), (), s32[]{:S(2)}) async-start(), calls=%async_computation.8 | async-start | bytes 884736
Sparse Core Ops, SparseCore 0:
  42.4 72.9 reduce-scatter.7
  163.0 37.4 reduce-scatter.5
  203.6 34.9 reduce-scatter.9
where the time goes:
time: 248 us; the launch traced here: 247 us
  waiting for transfers between devices  153 us (62%)
  local copies, waits for them, and re-layouts  36.5 us (15%)
  matrix products  22.8 us (9%)
  starting transfers between devices  18.1 us (7%)
  between operations  13.9 us (6%)
  other arithmetic  2.69 us (1%)
    all_to_all x1, waiting for transfers between devices, on_device(): lax.all_to_all(coef_buffer, 'aux', split_axis=0, concat_axis=0, tiled=True)  59.4 us
    unnamed x4, waiting for transfers between devices  36.6 us
    reduce_scatter x1, waiting for transfers between devices, on_device(): lax.psum_scatter(gamma_part, 'pair', scatter_dimension=1, tiled=True)  35.2 us
    all_to_all x1, waiting for transfers between devices, on_device(): lax.all_to_all(index_buffer, 'aux', split_axis=0, concat_axis=0, tiled=True)  21.5 us
    reshape x2, local copies, waits for them, and re-layouts, on_device(): coef_buffer = coef_buffer.reshape(n_aux, capacity, domain_rows, pno_rank)  10.3 us
    reshape x1, local copies, waits for them, and re-layouts, on_device(): pieces = back.reshape(received_count, aux_block, pao_dom, pao_block)  6.96 us
    dot_general x1, matrix products, on_device(): jnp.einsum('sxhy,shok->oxky', pieces, placement, preferred_element_type=j...  6.85 us
    all_to_all x1, starting transfers between devices, on_device(): lax.all_to_all(coef_buffer, 'aux', split_axis=0, concat_axis=0, tiled=True)  6.61 us
  transfers between devices with their start and end apart: 6, of which 4 were waited for; matrix products, arithmetic and copies ran while one was open for 23% of the time, Pallas kernels for 0%

commit v1 on v0

--- a/solution.py
+++ b/solution.py
@@ -1,15 +1,21 @@
+import functools
 import math
 
 import jax
 import jax.numpy as jnp
 from jax import lax
+from jax.experimental import pallas as pl
+from jax.experimental.pallas import tpu as pltpu
 from jax.sharding import PartitionSpec as P
 
 NBLK = 6
 ABPO = 4
-
-
-def on_device(integrals, amplitudes, pno_density, pno_coef, pao_blocks, aux_slice, aux_offset):
+MESH = pl.DeviceIdType.MESH
+TILE = 128
+SUB = 16
+
+
+def by_collectives(integrals, amplitudes, pno_density, pno_coef, pao_blocks, aux_slice, aux_offset):
     n_pair = lax.axis_size("pair")
     n_aux = lax.axis_size("aux")
     pair_count, domain_rows, pno_rank = pno_coef.shape
@@ -99,6 +105,292 @@
     return (aux_density, virtual_density * out_scale)
 
 
+def kernel(ints, amps, dens, coef, pao, aux, off, out, coef2, tri2, wei2, ids, lhs, rhs, own, c_send, c_recv,
+           ax_send, ax_recv, ay_send, ay_recv, by_send, by_recv, bx_send, bx_recv, keep1, keep2, cz_send, cz_recv,
+           cw_send, cw_recv, ck, pz_send, pz_recv, pw_send, pw_recv, cx_send, cx_recv, cy_send, cy_recv, ckx,
+           send_sems, recv_sems):
+    pairs, rows, rank = coef.shape
+    couples = pairs // 2
+    width = couples * TILE
+    unit = out.shape[0] // 3
+    lanes = out.shape[1]
+    p = lax.axis_index("pair")
+    z = lax.axis_index("aux")
+    c, x, y = p % 2, (p // 2) % 2, p // 4
+    z0, z1 = z % 2, z // 2
+    core = (p + 1 - 2 * c, z)
+    xdev = (p + 2 - 4 * x, z)
+    ydev = (p + 4 - 8 * y, z)
+    z0dev = (p, z + 1 - 2 * z0)
+    z1dev = (p, z + 2 - 4 * z1)
+
+    barrier = pltpu.get_barrier_semaphore()
+    for dev in (core, xdev, ydev, z0dev, z1dev):
+        pl.semaphore_signal(barrier, inc=1, device_id=dev, device_id_type=MESH)
+
+    started = []
+
+    def send(src, dst, dev):
+        n = len(started)
+        copy = pltpu.make_async_remote_copy(
+            src_ref=src, dst_ref=dst, send_sem=send_sems.at[n], recv_sem=recv_sems.at[n],
+            device_id=dev, device_id_type=MESH)
+        copy.start()
+        started.append(copy)
+        return copy
+
+    low = lax.broadcasted_iota(jnp.int32, (SUB, TILE), 1) < rank
+    for q in range(couples):
+        at = slice(q * TILE, (q + 1) * TILE)
+        for h in range(2):
+            ids[h, :, at] = jnp.where(low, pao[2 * q, h], pao[2 * q + 1, h])
+            ids[2 + h, :, at] = jnp.where(
+                low,
+                aux[2 * q, h] * ABPO + off[2 * q, h],
+                aux[2 * q + 1, h] * ABPO + off[2 * q + 1, h])
+
+    zero = jnp.zeros((rank, rank), jnp.bfloat16)
+
+    def diag(ref, q):
+        return jnp.concatenate(
+            [jnp.concatenate([ref[2 * q], zero], 1), jnp.concatenate([zero, ref[2 * q + 1]], 1)], 0)
+
+    def prepare(q, carry):
+        at = pl.ds(pl.multiple_of(q * TILE, TILE), TILE)
+        both = jnp.concatenate([coef[2 * q], coef[2 * q + 1]], 1)
+        coef2[:, at] = both
+        wei2[:, at] = jnp.dot(both, diag(dens, q), preferred_element_type=jnp.float32).astype(jnp.bfloat16)
+        both = jnp.concatenate([ints[2 * q], ints[2 * q + 1]], 1)
+        tri2[:, at] = jnp.dot(both, diag(amps, q), preferred_element_type=jnp.float32).astype(jnp.bfloat16)
+        return carry
+
+    lax.fori_loop(0, couples, prepare, 0)
+
+    def mask(row, value):
+        return jnp.where(ids[row] == value, 1.0, 0.0).astype(jnp.bfloat16)
+
+    half_rows = rows // 2
+
+    def place(dst, dst_row, src, src_row, count, first, value):
+        m0, m1 = mask(first, value), mask(first + 1, value)
+        for r in range(0, count, SUB):
+            a = src[pl.ds(pl.multiple_of(src_row + r, SUB), SUB), :]
+            b = src[pl.ds(pl.multiple_of(src_row + half_rows + r, SUB), SUB), :]
+            dst[pl.ds(pl.multiple_of(dst_row + r, SUB), SUB), :] = a * m0 + b * m1
+
+    per_block = half_rows // unit
+
+    def lhs_unit(n, carry):
+        half, g, i, j = n // 12, (n // 4) % 3, (n // 2) % 2, n % 2
+        is_b = jnp.where(g == 1, 1, 0)
+        si = is_b * j + (1 - is_b) * i
+        sj = is_b * i + (1 - is_b) * j
+        cc = (1 - half) * (1 - c) + half * c
+        xx = (1 - si) * (1 - x) + si * x
+        yy = (1 - sj) * (1 - y) + sj * y
+        u = ((yy * 2 + xx) * 2 + cc) * 3 + g
+        place(lhs, n * unit, coef2, (u % per_block) * unit, unit, 0, u // per_block)
+        return carry
+
+    lax.fori_loop(0, 24, lhs_unit, 0)
+
+    chunk_of = ((1 - z1) * 2 + 1 - z0, (1 - z1) * 2 + z0, z1 * 2 + 1 - z0, z)
+
+    def build(step):
+        k = chunk_of[step]
+        buf = rhs.at[step % 2]
+
+        def aux_tile(j, carry):
+            place(buf, j * TILE, tri2, 0, TILE, 2, k * ABPO + j)
+            return carry
+
+        def virt_tile(j, carry):
+            place(buf, (ABPO + j) * TILE, wei2, 0, TILE, 0, 3 * (k // 2) + k % 2 + j)
+            return carry
+
+        lax.fori_loop(0, ABPO, aux_tile, 0)
+        lax.fori_loop(0, 2, virt_tile, 0)
+
+    n_rows = 12 * unit
+    wide = 2 * TILE
+
+    def product(step, half, dst, kind):
+        left = lhs.at[pl.ds(half * n_rows, n_rows)]
+
+        def body(t, carry):
+            at = pl.ds(pl.multiple_of(t * wide, wide), wide)
+            dst[:, at] = lax.dot_general(
+                left[...], rhs[step % 2, at, :], (((1,), (1,)), ((), ())),
+                preferred_element_type=jnp.float32).astype(kind)
+            return carry
+
+        lax.fori_loop(0, lanes // wide, body, 0)
+
+    f32, bf16 = jnp.float32, jnp.bfloat16
+    u2, u4 = 2 * unit, 4 * unit
+    stage1 = {}
+    stage2 = {}
+    zcopy = {}
+
+    def first(step):
+        stage1[step, "c"].wait_recv()
+
+        def summed(lo, hi):
+            return own[lo:hi, :] + c_recv[step, lo:hi, :].astype(f32)
+
+        ax_send[step] = summed(0, u2).astype(bf16)
+        stage1[step, "a"] = send(ax_send.at[step], ax_recv.at[step], xdev)
+        by_send[step] = summed(u4, u4 + u2).astype(bf16)
+        stage1[step, "b"] = send(by_send.at[step], by_recv.at[step], ydev)
+        if step in (0, 2):
+            cz_send[step // 2] = summed(2 * u4, 3 * u4).astype(bf16)
+            zcopy["c", step] = send(cz_send.at[step // 2], cz_recv.at[step // 2], z0dev)
+        else:
+            ck[step // 2] = summed(2 * u4, 3 * u4)
+        keep1[step, 0:u2] = summed(u2, u4)
+        keep1[step, u2:u4] = summed(u4 + u2, 2 * u4)
+
+    def second(step):
+        stage1[step, "a"].wait_recv()
+        ay_send[step] = (keep1[step, 0:unit] + ax_recv[step, 0:unit].astype(f32)).astype(bf16)
+        stage2[step, "a"] = send(ay_send.at[step], ay_recv.at[step], ydev)
+        keep2[step, 0:unit] = keep1[step, unit:u2] + ax_recv[step, unit:u2].astype(f32)
+        stage1[step, "b"].wait_recv()
+        bx_send[step] = (keep1[step, u2:u2 + unit] + by_recv[step, 0:unit].astype(f32)).astype(bf16)
+        stage2[step, "b"] = send(bx_send.at[step], bx_recv.at[step], xdev)
+        keep2[step, unit:u2] = keep1[step, u2 + unit:u4] + by_recv[step, unit:u2].astype(f32)
+
+    def third_sum(step, lo, hi):
+        got = ay_recv if lo == 0 else bx_recv
+        return keep2[step, lo:hi] + got[step].astype(f32)
+
+    def third(step):
+        stage2[step, "a"].wait_recv()
+        stage2[step, "b"].wait_recv()
+        halves = ((0, unit), (unit, u2))
+        if step in (0, 2):
+            for lo, hi in halves:
+                pz_send[step // 2, lo:hi] = third_sum(step, lo, hi).astype(bf16)
+            zcopy["p", step] = send(pz_send.at[step // 2], pz_recv.at[step // 2], z0dev)
+        elif step == 1:
+            zcopy["p", 0].wait_recv()
+            for lo, hi in halves:
+                pw_send[lo:hi] = (third_sum(step, lo, hi) + pz_recv[0, lo:hi].astype(f32)).astype(bf16)
+            zcopy["p", 1] = send(pw_send, pw_recv, z1dev)
+        else:
+            zcopy["p", 2].wait_recv()
+            zcopy["p", 1].wait_recv()
+            for lo, hi in halves:
+                out[lo:hi] = third_sum(step, lo, hi) + pz_recv[1, lo:hi].astype(f32) + pw_recv[lo:hi].astype(f32)
+
+    def c_across():
+        zcopy["c", 0].wait_recv()
+        cw_send[...] = (ck[0] + cz_recv[0].astype(f32)).astype(bf16)
+        zcopy["c", 1] = send(cw_send, cw_recv, z1dev)
+
+    build(0)
+    for step in range(4):
+        product(step, 0, c_send.at[step], bf16)
+        if step == 0:
+            pl.semaphore_wait(barrier, 5)
+        stage1[step, "c"] = send(c_send.at[step], c_recv.at[step], core)
+        product(step, 1, own, f32)
+        if step < 3:
+            build(step + 1)
+        first(step)
+        if step >= 1:
+            second(step - 1)
+        if step == 1:
+            c_across()
+        if step >= 2:
+            third(step - 2)
+
+    second(3)
+    third(2)
+    zcopy["c", 2].wait_recv()
+    zcopy["c", 1].wait_recv()
+
+    def c_sum(lo, hi):
+        return ck[1, lo:hi] + cz_recv[1, lo:hi].astype(f32) + cw_recv[lo:hi].astype(f32)
+
+    cx_send[...] = c_sum(0, u2).astype(bf16)
+    cx = send(cx_send, cx_recv, xdev)
+    ckx[...] = c_sum(u2, u4)
+    third(3)
+    cx.wait_recv()
+    cy_send[...] = (ckx[0:unit] + cx_recv[0:unit].astype(f32)).astype(bf16)
+    cy = send(cy_send, cy_recv, ydev)
+    ckx[unit:u2] = ckx[unit:u2] + cx_recv[unit:u2].astype(f32)
+    cy.wait_recv()
+    out[u2:3 * unit] = ckx[unit:u2] + cy_recv[...].astype(f32)
+    for copy in started:
+        copy.wait_send()
+
+
+COPIES = 4 + 8 + 8 + 2 + 1 + 2 + 1 + 2
+
+
+def by_kernel(integrals, amplitudes, pno_density, pno_coef, pao_blocks, aux_slice, aux_offset):
+    n_pair = lax.axis_size("pair")
+    n_aux = lax.axis_size("aux")
+    pairs, rows, rank = pno_coef.shape
+    block = rows // pao_blocks.shape[1]
+    ao_count = NBLK * block
+    shard = ao_count // n_pair
+    unit = shard // 3
+    aux_lanes = ABPO * block
+    lanes = aux_lanes + 2 * block
+    width = pairs * rank
+    scale = 1.0 / math.sqrt(pairs * n_pair)
+    vmem = pl.BlockSpec(memory_space=pltpu.VMEM)
+    smem = pl.BlockSpec(memory_space=pltpu.SMEM)
+
+    def half(*dims):
+        return pltpu.VMEM(dims + (lanes,), jnp.bfloat16)
+
+    def full(*dims):
+        return pltpu.VMEM(dims + (lanes,), jnp.float32)
+
+    u1, u2, u4 = unit, 2 * unit, 4 * unit
+    out = pl.pallas_call(
+        kernel,
+        out_shape=jax.ShapeDtypeStruct((shard, lanes), jnp.float32),
+        in_specs=[vmem] * 4 + [smem] * 3,
+        out_specs=vmem,
+        scratch_shapes=[
+            pltpu.VMEM((rows, width), jnp.bfloat16),
+            pltpu.VMEM((rows, width), jnp.bfloat16),
+            pltpu.VMEM((rows, width), jnp.bfloat16),
+            pltpu.VMEM((4, SUB, width), jnp.int32),
+            pltpu.VMEM((24 * unit, width), jnp.bfloat16),
+            pltpu.VMEM((2, lanes, width), jnp.bfloat16),
+            full(12 * unit),
+            half(4, 12 * unit), half(4, 12 * unit),
+            half(4, u2), half(4, u2), half(4, u1), half(4, u1),
+            half(4, u2), half(4, u2), half(4, u1), half(4, u1),
+            full(4, u4), full(4, u2),
+            half(2, u4), half(2, u4), half(u4), half(u4), full(2, u4),
+            half(2, u2), half(2, u2), half(u2), half(u2),
+            half(u2), half(u2), half(u1), half(u1), full(u2),
+            pltpu.SemaphoreType.DMA((COPIES,)),
+            pltpu.SemaphoreType.DMA((COPIES,)),
+        ],
+        compiler_params=pltpu.CompilerParams(
+            collective_id=0, has_side_effects=True, vmem_limit_bytes=60 * 1024 * 1024),
+    )(integrals, amplitudes, pno_density, pno_coef, pao_blocks, aux_slice, aux_offset)
+    strip = ao_count // n_aux
+    start = (lax.axis_index("aux") % 2) * (2 * block - strip)
+    virt = lax.dynamic_slice(out, (0, aux_lanes + start), (shard, strip))
+    return out[:, :aux_lanes].T * scale, virt.T * scale
+
+
+def on_device(*args):
+    pairs, rows, rank = args[3].shape
+    fits = lax.axis_size("pair") == 8 and lax.axis_size("aux") == 4 and pairs % 2 == 0 and 2 * rank == TILE
+    fits = fits and rows == 2 * TILE and args[0].shape[1] == 2 * TILE
+    return by_kernel(*args) if fits else by_collectives(*args)
+
+
 def solution(mesh):
     in_specs = (
         P(("pair", "aux"), None, None),

time: 248 us -> 53.9 us (0.22)
  waiting for transfers between devices: 153 us -> 0 us
  Pallas kernels: 0 us -> 43.8 us
  local copies, waits for them, and re-layouts: 36.5 us -> 6.57 us
  matrix products: 22.8 us -> 0 us
  starting transfers between devices: 18.1 us -> 0 us
  between operations: 13.9 us -> 0.66 us
    all_to_all x3 -> x0, waiting for transfers between devices: 80.9 us -> none  [the longest x1 59.4 us: on_device(): lax.all_to_all(coef_buffer, 'aux', split_axis=0, concat_axis=0, tiled=True)]
    pallas_call x0 -> x1, Pallas kernels: none -> 43.8 us  [by_kernel(): pl.pallas_call(kernel, out_shape=jax.ShapeDtypeStruct((shard, lanes), jnp...]
    unnamed x4 -> x0, waiting for transfers between devices: 36.6 us -> none
    reduce_scatter x2 -> x0, waiting for transfers between devices: 35.3 us -> none  [the longest x1 35.2 us: on_device(): lax.psum_scatter(gamma_part, 'pair', scatter_dimension=1, tiled=True)]
    reshape x16 -> x0, local copies, waits for them, and re-layouts: 29.4 us -> none  [the longest x2 10.3 us: on_device(): coef_buffer = coef_buffer.reshape(n_aux, capacity, domain_rows, pno_rank)]
    dot_general x10 -> x0, matrix products: 22.8 us -> none  [the longest x1 6.85 us: on_device(): jnp.einsum('sxhy,shok->oxky', pieces, placement, preferred_element_type=j...]
    all_to_all x3 -> x0, starting transfers between devices: 18.1 us -> none  [the longest x1 6.61 us: on_device(): lax.all_to_all(coef_buffer, 'aux', split_axis=0, concat_axis=0, tiled=True)]
    unnamed x17 -> x14, local copies, waits for them, and re-layouts: 5.74 us -> 6.57 us
  transfers between devices with their start and end apart: 6 -> 0, of which waited for: 4 -> 0; matrix products, arithmetic and copies ran while one was open for 23% -> 0% of each run, Pallas kernels for 0% -> 0%
where the time goes in v1:
time: 53.9 us; the launch traced here: 53.6 us
  Pallas kernels  43.8 us (81%)
  local copies, waits for them, and re-layouts  6.57 us (12%)
  other arithmetic  2.6 us (5%)
  between operations  0.66 us (1%)
    pallas_call x1, Pallas kernels, by_kernel(): pl.pallas_call(kernel, out_shape=jax.ShapeDtypeStruct((shard, lanes), jnp...  43.8 us
    unnamed x14, local copies, waits for them, and re-layouts  6.57 us
    mul x2, other arithmetic, by_kernel(): return (out[:, :aux_lanes].T * scale, virt.T * scale)  2.6 us

profile of v1, /device:TPU:0, one launch (start us, length us, event | category | flops | bytes accessed | tf_op | source)
XLA Modules:
  0.0 53.6 jit_solution(12691316249516253957)
XLA Ops:
  0.6 0.0 copy-start
  0.6 2.4 %copy.9.ints = bf16[16,256,64]{2,1,0:T(8,128)(2,1)} copy(bf16[16,256,64]{1,2,0:T(8,128)(2,1)} %param.7) | data formatting | bytes 1048576 | tf_op args[0]
  3.1 0.0 copy-done
  3.1 0.0 copy-start.1
  3.1 1.4 %copy.10.coef = bf16[16,256,64]{2,1,0:T(8,128)(2,1)} copy(bf16[16,256,64]{1,2,0:T(8,128)(2,1)S(1)} %copy-done) | data formatting | bytes 1048576 | tf_op args[3]
  4.4 0.0 copy-done.1
  4.4 0.0 copy-start.2
  4.4 0.7 %copy.11.pao = s32[16,2]{1,0:T(8,128)} copy(s32[16,2]{0,1:T(2,128)S(1)} %copy-done.1) | data formatting | bytes 256 | tf_op args[4]
  5.1 0.0 copy-done.2
  5.1 0.0 copy-start.3
  5.1 0.7 %copy.12.aux = s32[16,2]{1,0:T(8,128)} copy(s32[16,2]{0,1:T(2,128)S(1)} %copy-done.2) | data formatting | bytes 256 | tf_op args[5]
  5.8 0.0 copy-done.3
  5.8 0.7 %copy.13.off = s32[16,2]{1,0:T(8,128)} copy(s32[16,2]{0,1:T(2,128)S(1)} %copy-done.3) | data formatting | bytes 256 | tf_op args[6]
  6.5 43.8 %shard_map.86 = f32[96,768]{1,0:T(8,128)} custom-call(bf16[16,256,64]{2,1,0:T(8,128)(2,1)} %copy.9.ints, bf16[16,64,64]{2,1,0:T(8,128)(2,1)} %amps.1, bf16[16,64,64]{2,1,0:T(8,128)(2,1)} %dens.1, bf16[16,256,64]{2,1,0:T(8,128)(2,1)} %copy.10.coef, s32[16,2]{1,0:T(8,128)} %copy.11.pao, s32[16,2]{1,0:T(8,128)} %copy.12.aux, s32[16,2]{1,0:T(8,128)} %copy.13.off), custom_call_target="tpu_custom_call" | custom-call | tf_op jit(solution)/shard_map/pallas_call | solution.py:355
  50.3 1.6 %multiply_bitcast_fusion = f32[512,96]{0,1:T(8,128)} fusion(f32[96,768]{1,0:T(8,128)} %shard_map.86), kind=kLoop, calls=%fused_computation | loop fusion | flops 49152 | bytes 393216 | tf_op jit(solution)/shard_map/mul | solution.py:384
  51.9 1.0 %multiply_bitcast_fusion.1 = f32[192,96]{0,1:T(8,128)S(1)} fusion(f32[96,768]{1,0:T(8,128)} %shard_map.86, s32[]{:T(128)S(6)} %select_n.11), kind=kLoop, calls=%fused_computation.1 | loop fusion | flops 18432 | bytes 147460 | tf_op jit(solution)/shard_map/mul | solution.py:384
  52.9 0.7 %copy.14 = f32[192,96]{1,0:T(8,128)} copy(f32[192,96]{0,1:T(8,128)S(1)} %multiply_bitcast_fusion.1) | data formatting | bytes 147456
Async XLA Ops:
  0.6 2.4 %copy-start = (bf16[16,256,64]{1,2,0:T(8,128)(2,1)S(1)}, bf16[16,256,64]{1,2,0:T(8,128)(2,1)}, u32[]{:S(2)}) copy-start(bf16[16,256,64]{1,2,0:T(8,128)(2,1)} %param.10) | copy-start | bytes 1572868
  3.1 1.4 %copy-start.1 = (s32[16,2]{0,1:T(2,128)S(1)}, s32[16,2]{0,1:T(2,128)}, u32[]{:S(2)}) copy-start(s32[16,2]{0,1:T(2,128)} %param.11) | copy-start | bytes 388
  4.4 0.7 %copy-start.2 = (s32[16,2]{0,1:T(2,128)S(1)}, s32[16,2]{0,1:T(2,128)}, u32[]{:S(2)}) copy-start(s32[16,2]{0,1:T(2,128)} %param.12) | copy-start | bytes 388
  5.1 0.7 %copy-start.3 = (s32[16,2]{0,1:T(2,128)S(1)}, s32[16,2]{0,1:T(2,128)}, u32[]{:S(2)}) copy-start(s32[16,2]{0,1:T(2,128)} %param.13) | copy-start | bytes 388

commit v2 on v1

--- a/solution.py
+++ b/solution.py
@@ -105,14 +105,13 @@
     return (aux_density, virtual_density * out_scale)
 
 
-def kernel(ints, amps, dens, coef, pao, aux, off, out, coef2, tri2, wei2, ids, lhs, rhs, own, c_send, c_recv,
+def kernel(scale, ints, amps, dens, coef, pao, aux, off, gamma, virt, out, coef2, tri2, wei2, ids, lhs, rhs, own, c_send, c_recv,
            ax_send, ax_recv, ay_send, ay_recv, by_send, by_recv, bx_send, bx_recv, keep1, keep2, cz_send, cz_recv,
-           cw_send, cw_recv, ck, pz_send, pz_recv, pw_send, pw_recv, cx_send, cx_recv, cy_send, cy_recv, ckx,
+           cw_send, cw_recv, ck, pz_send, pz_recv, pw_send, pw_recv, cx_send, cx_recv, cy_send, cy_recv, ckx, turned,
            send_sems, recv_sems):
-    pairs, rows, rank = coef.shape
+    pairs, rank, rows = coef.shape
     couples = pairs // 2
-    width = couples * TILE
-    unit = out.shape[0] // 3
+    unit = gamma.shape[0] // 3
     lanes = out.shape[1]
     p = lax.axis_index("pair")
     z = lax.axis_index("aux")
@@ -143,28 +142,22 @@
     for q in range(couples):
         at = slice(q * TILE, (q + 1) * TILE)
         for h in range(2):
-            ids[h, :, at] = jnp.where(low, pao[2 * q, h], pao[2 * q + 1, h])
-            ids[2 + h, :, at] = jnp.where(
-                low,
-                aux[2 * q, h] * ABPO + off[2 * q, h],
-                aux[2 * q + 1, h] * ABPO + off[2 * q + 1, h])
+            ids[h, :, at] = jnp.where(low, pao[h, 2 * q], pao[h, 2 * q + 1])
 
     zero = jnp.zeros((rank, rank), jnp.bfloat16)
 
-    def diag(ref, q):
-        return jnp.concatenate(
+    def mixed(ref, q, both):
+        diag = jnp.concatenate(
             [jnp.concatenate([ref[2 * q], zero], 1), jnp.concatenate([zero, ref[2 * q + 1]], 1)], 0)
-
-    def prepare(q, carry):
-        at = pl.ds(pl.multiple_of(q * TILE, TILE), TILE)
-        both = jnp.concatenate([coef[2 * q], coef[2 * q + 1]], 1)
-        coef2[:, at] = both
-        wei2[:, at] = jnp.dot(both, diag(dens, q), preferred_element_type=jnp.float32).astype(jnp.bfloat16)
-        both = jnp.concatenate([ints[2 * q], ints[2 * q + 1]], 1)
-        tri2[:, at] = jnp.dot(both, diag(amps, q), preferred_element_type=jnp.float32).astype(jnp.bfloat16)
-        return carry
-
-    lax.fori_loop(0, couples, prepare, 0)
+        return lax.dot_general(
+            diag, both, (((0,), (0,)), ((), ())), preferred_element_type=jnp.float32).astype(jnp.bfloat16)
+
+    for q in range(couples):
+        at = slice(q * TILE, (q + 1) * TILE)
+        both = coef[2 * q:2 * q + 2].reshape(2 * rank, rows)
+        coef2[:, at] = both.T
+        wei2[at, :] = mixed(dens, q, both)
+        tri2[at, :] = mixed(amps, q, ints[2 * q:2 * q + 2].reshape(2 * rank, rows))
 
     def mask(row, value):
         return jnp.where(ids[row] == value, 1.0, 0.0).astype(jnp.bfloat16)
@@ -198,18 +191,24 @@
 
     def build(step):
         k = chunk_of[step]
-        buf = rhs.at[step % 2]
-
-        def aux_tile(j, carry):
-            place(buf, j * TILE, tri2, 0, TILE, 2, k * ABPO + j)
+        virt_first = 3 * (k // 2) + k % 2
+
+        def switch(label, value):
+            return jnp.full((rank, TILE), jnp.where(label == value, 1.0, 0.0), jnp.float32).astype(jnp.bfloat16)
+
+        def one_pair(n, carry):
+            at = pl.ds(pl.multiple_of(n * rank, rank), rank)
+            for src, blocks, labels, start, base in (
+                (tri2, ABPO, [aux[h, n] * ABPO + off[h, n] for h in range(2)], k * ABPO, 0),
+                (wei2, 2, [pao[h, n] for h in range(2)], virt_first, ABPO),
+            ):
+                low_part, high_part = src[at, 0:TILE], src[at, TILE:2 * TILE]
+                for j in range(blocks):
+                    rhs[step % 2, at, (base + j) * TILE:(base + j + 1) * TILE] = (
+                        low_part * switch(labels[0], start + j) + high_part * switch(labels[1], start + j))
             return carry
 
-        def virt_tile(j, carry):
-            place(buf, (ABPO + j) * TILE, wei2, 0, TILE, 0, 3 * (k // 2) + k % 2 + j)
-            return carry
-
-        lax.fori_loop(0, ABPO, aux_tile, 0)
-        lax.fori_loop(0, 2, virt_tile, 0)
+        lax.fori_loop(0, pairs, one_pair, 0, unroll=2)
 
     n_rows = 12 * unit
     wide = 2 * TILE
@@ -220,7 +219,7 @@
         def body(t, carry):
             at = pl.ds(pl.multiple_of(t * wide, wide), wide)
             dst[:, at] = lax.dot_general(
-                left[...], rhs[step % 2, at, :], (((1,), (1,)), ((), ())),
+                left[...], rhs[step % 2, :, at], (((1,), (0,)), ((), ())),
                 preferred_element_type=jnp.float32).astype(kind)
             return carry
 
@@ -323,6 +322,12 @@
     ckx[unit:u2] = ckx[unit:u2] + cx_recv[unit:u2].astype(f32)
     cy.wait_recv()
     out[u2:3 * unit] = ckx[unit:u2] + cy_recv[...].astype(f32)
+    aux_lanes = gamma.shape[1]
+    gamma[...] = out[0:3 * unit, 0:aux_lanes] * scale
+    out[3 * unit:] = jnp.zeros((out.shape[0] - 3 * unit, lanes), f32)
+    turned[...] = out[:, aux_lanes:].T * scale
+    strip = virt.shape[0]
+    virt[...] = turned[pl.ds(pl.multiple_of(z0 * (turned.shape[0] - strip), 8), strip), 0:3 * unit]
     for copy in started:
         copy.wait_send()
 
@@ -352,18 +357,22 @@
         return pltpu.VMEM(dims + (lanes,), jnp.float32)
 
     u1, u2, u4 = unit, 2 * unit, 4 * unit
-    out = pl.pallas_call(
-        kernel,
-        out_shape=jax.ShapeDtypeStruct((shard, lanes), jnp.float32),
+    gamma, virt = pl.pallas_call(
+        functools.partial(kernel, scale),
+        out_shape=[
+            jax.ShapeDtypeStruct((shard, aux_lanes), jnp.float32),
+            jax.ShapeDtypeStruct((ao_count // n_aux, shard), jnp.float32),
+        ],
         in_specs=[vmem] * 4 + [smem] * 3,
-        out_specs=vmem,
+        out_specs=[vmem] * 2,
         scratch_shapes=[
+            full(TILE),
             pltpu.VMEM((rows, width), jnp.bfloat16),
-            pltpu.VMEM((rows, width), jnp.bfloat16),
-            pltpu.VMEM((rows, width), jnp.bfloat16),
-            pltpu.VMEM((4, SUB, width), jnp.int32),
+            pltpu.VMEM((width, rows), jnp.bfloat16),
+            pltpu.VMEM((width, rows), jnp.bfloat16),
+            pltpu.VMEM((2, SUB, width), jnp.int32),
             pltpu.VMEM((24 * unit, width), jnp.bfloat16),
-            pltpu.VMEM((2, lanes, width), jnp.bfloat16),
+            pltpu.VMEM((2, width, lanes), jnp.bfloat16),
             full(12 * unit),
             half(4, 12 * unit), half(4, 12 * unit),
             half(4, u2), half(4, u2), half(4, u1), half(4, u1),
@@ -372,16 +381,15 @@
             half(2, u4), half(2, u4), half(u4), half(u4), full(2, u4),
             half(2, u2), half(2, u2), half(u2), half(u2),
             half(u2), half(u2), half(u1), half(u1), full(u2),
+            pltpu.VMEM((2 * block, TILE), jnp.float32),
             pltpu.SemaphoreType.DMA((COPIES,)),
             pltpu.SemaphoreType.DMA((COPIES,)),
         ],
         compiler_params=pltpu.CompilerParams(
             collective_id=0, has_side_effects=True, vmem_limit_bytes=60 * 1024 * 1024),
-    )(integrals, amplitudes, pno_density, pno_coef, pao_blocks, aux_slice, aux_offset)
-    strip = ao_count // n_aux
-    start = (lax.axis_index("aux") % 2) * (2 * block - strip)
-    virt = lax.dynamic_slice(out, (0, aux_lanes + start), (shard, strip))
-    return out[:, :aux_lanes].T * scale, virt.T * scale
+    )(integrals.swapaxes(1, 2), amplitudes, pno_density, pno_coef.swapaxes(1, 2),
+      pao_blocks.T, aux_slice.T, aux_offset.T)
+    return gamma.T, virt
 
 
 def on_device(*args):

time: 53.9 us -> 45.6 us (0.85)
  local copies, waits for them, and re-layouts: 6.57 us -> 2.29 us
  other arithmetic: 2.6 us -> 0 us
  Pallas kernels: 43.8 us -> 42.5 us
    unnamed x14 -> x4, local copies, waits for them, and re-layouts: 6.57 us -> 2.29 us
    mul x2 -> x0, other arithmetic: 2.6 us -> none  [by_kernel(): return (out[:, :aux_lanes].T * scale, virt.T * scale)]
    pallas_call x1, Pallas kernels: 43.8 us -> 42.5 us  [by_kernel(): pl.pallas_call(functools.partial(kernel, scale), out_shape=[jax.ShapeDtyp...]
where the time goes in v2:
time: 45.6 us; the launch traced here: 45.5 us
  Pallas kernels  42.5 us (93%)
  local copies, waits for them, and re-layouts  2.29 us (5%)
  between operations  0.65 us (1%)
    pallas_call x1, Pallas kernels, by_kernel(): pl.pallas_call(functools.partial(kernel, scale), out_shape=[jax.ShapeDtyp...  42.5 us
    unnamed x4, local copies, waits for them, and re-layouts  2.29 us

profile of v2, /device:TPU:0, one launch (start us, length us, event | category | flops | bytes accessed | tf_op | source)
XLA Modules:
  0.0 45.5 jit_solution(3063224002782035158)
XLA Ops:
  0.6 42.5 %shard_map.86 = (f32[96,512]{1,0:T(8,128)}, f32[192,96]{1,0:T(8,128)}) custom-call(bf16[16,64,256]{2,1,0:T(8,128)(2,1)} %bitcast.6, bf16[16,64,64]{2,1,0:T(8,128)(2,1)} %amps.1, bf16[16,64,64]{2,1,0:T(8,128)(2,1)} %dens.1, bf16[16,64,256]{2,1,0:T(8,128)(2,1)} %bitcast.7, s32[2,16]{1,0:T(2,128)} %bitcast.9, s32[2,16]{1,0:T(2,128)} %bitcast.10, s32[2,16]{1,0:T(2,128)} %bitcast.11), custom_call_target="tpu_custom_call" | custom-call | tf_op jit(solution)/shard_map/pallas_call | solution.py:360
  43.2 0.0 copy-start
  43.2 1.6 %copy.11 = f32[512,96]{0,1:T(8,128)} copy(f32[512,96]{0,1:T(8,128)} %bitcast.8) | data formatting | bytes 393216
  44.8 0.0 copy-done
  44.8 0.6 %copy.12 = f32[192,96]{1,0:T(8,128)} copy(f32[192,96]{1,0:T(8,128)S(1)} %copy-done) | data formatting | bytes 147456
Async XLA Ops:
  43.2 1.7 %copy-start = (f32[192,96]{1,0:T(8,128)S(1)}, f32[192,96]{1,0:T(8,128)}, u32[]{:S(2)}) copy-start(f32[192,96]{1,0:T(8,128)} %get-tuple-element.9) | copy-start | bytes 221188

commit v3 on v2

--- a/solution.py
+++ b/solution.py
@@ -105,13 +105,22 @@
     return (aux_density, virtual_density * out_scale)
 
 
+def group_rows(shard):
+    units = shard // SUB
+    c = max(1, units // 6)
+    a = units // 2
+    return a * SUB, (units - a - c) * SUB, c * SUB
+
+
 def kernel(scale, ints, amps, dens, coef, pao, aux, off, gamma, virt, out, coef2, tri2, wei2, ids, lhs, rhs, own, c_send, c_recv,
            ax_send, ax_recv, ay_send, ay_recv, by_send, by_recv, bx_send, bx_recv, keep1, keep2, cz_send, cz_recv,
            cw_send, cw_recv, ck, pz_send, pz_recv, pw_send, pw_recv, cx_send, cx_recv, cy_send, cy_recv, ckx, turned,
            send_sems, recv_sems):
     pairs, rank, rows = coef.shape
     couples = pairs // 2
-    unit = gamma.shape[0] // 3
+    shard = gamma.shape[0]
+    na, nb, nc = group_rows(shard)
+    nab = na + nb
     lanes = out.shape[1]
     p = lax.axis_index("pair")
     z = lax.axis_index("aux")
@@ -171,21 +180,22 @@
             b = src[pl.ds(pl.multiple_of(src_row + half_rows + r, SUB), SUB), :]
             dst[pl.ds(pl.multiple_of(dst_row + r, SUB), SUB), :] = a * m0 + b * m1
 
-    per_block = half_rows // unit
-
-    def lhs_unit(n, carry):
-        half, g, i, j = n // 12, (n // 4) % 3, (n // 2) % 2, n % 2
-        is_b = jnp.where(g == 1, 1, 0)
-        si = is_b * j + (1 - is_b) * i
-        sj = is_b * i + (1 - is_b) * j
-        cc = (1 - half) * (1 - c) + half * c
-        xx = (1 - si) * (1 - x) + si * x
-        yy = (1 - sj) * (1 - y) + sj * y
-        u = ((yy * 2 + xx) * 2 + cc) * 3 + g
-        place(lhs, n * unit, coef2, (u % per_block) * unit, unit, 0, u // per_block)
-        return carry
-
-    lax.fori_loop(0, 24, lhs_unit, 0)
+    for count, base, offset, y_first in ((na, 0, 0, 0), (nb, 4 * na, na, 1), (nc, 4 * nab, nab, 0)):
+
+        def lhs_unit(n, carry, count=count, base=base, offset=offset, y_first=y_first):
+            pieces = count // SUB
+            half, ij, t = n // (4 * pieces), (n // pieces) % 4, n % pieces
+            i, j = ij // 2, ij % 2
+            si, sj = (j, i) if y_first else (i, j)
+            cc = (1 - half) * (1 - c) + half * c
+            xx = (1 - si) * (1 - x) + si * x
+            yy = (1 - sj) * (1 - y) + sj * y
+            row = ((yy * 2 + xx) * 2 + cc) * shard + offset + t * SUB
+            place(lhs, half * (4 * shard) + base + (ij * pieces + t) * SUB, coef2,
+                  row % half_rows, SUB, 0, row // half_rows)
+            return carry
+
+        lax.fori_loop(0, 8 * (count // SUB), lhs_unit, 0)
 
     chunk_of = ((1 - z1) * 2 + 1 - z0, (1 - z1) * 2 + z0, z1 * 2 + 1 - z0, z)
 
@@ -210,7 +220,7 @@
 
         lax.fori_loop(0, pairs, one_pair, 0, unroll=2)
 
-    n_rows = 12 * unit
+    n_rows = 4 * shard
     wide = 2 * TILE
 
     def product(step, half, dst, kind):
@@ -226,10 +236,11 @@
         lax.fori_loop(0, lanes // wide, body, 0)
 
     f32, bf16 = jnp.float32, jnp.bfloat16
-    u2, u4 = 2 * unit, 4 * unit
     stage1 = {}
     stage2 = {}
     zcopy = {}
+    to_b, to_c = 4 * na, 4 * nab
+    a_dev, b_dev = (xdev, ydev), (ydev, xdev)
 
     def first(step):
         stage1[step, "c"].wait_recv()
@@ -237,36 +248,48 @@
         def summed(lo, hi):
             return own[lo:hi, :] + c_recv[step, lo:hi, :].astype(f32)
 
-        ax_send[step] = summed(0, u2).astype(bf16)
-        stage1[step, "a"] = send(ax_send.at[step], ax_recv.at[step], xdev)
-        by_send[step] = summed(u4, u4 + u2).astype(bf16)
-        stage1[step, "b"] = send(by_send.at[step], by_recv.at[step], ydev)
+        def quarters(base, count):
+            order = (0, 1, 2, 3) if step % 2 == 0 else (0, 2, 1, 3)
+            return [summed(base + n * count, base + (n + 1) * count) for n in order]
+
+        a_parts, b_parts = quarters(0, na), quarters(to_b, nb)
+        ax_send[step, 0:na] = a_parts[0].astype(bf16)
+        ax_send[step, na:2 * na] = a_parts[1].astype(bf16)
+        stage1[step, "a"] = send(ax_send.at[step], ax_recv.at[step], a_dev[step % 2])
+        by_send[step, 0:nb] = b_parts[0].astype(bf16)
+        by_send[step, nb:2 * nb] = b_parts[1].astype(bf16)
+        stage1[step, "b"] = send(by_send.at[step], by_recv.at[step], b_dev[step % 2])
         if step in (0, 2):
-            cz_send[step // 2] = summed(2 * u4, 3 * u4).astype(bf16)
+            cz_send[step // 2] = summed(to_c, to_c + 4 * nc).astype(bf16)
             zcopy["c", step] = send(cz_send.at[step // 2], cz_recv.at[step // 2], z0dev)
         else:
-            ck[step // 2] = summed(2 * u4, 3 * u4)
-        keep1[step, 0:u2] = summed(u2, u4)
-        keep1[step, u2:u4] = summed(u4 + u2, 2 * u4)
+            ck[step // 2] = summed(to_c, to_c + 4 * nc)
+        mid = 2 * na
+        keep1[step, 0:na] = a_parts[2]
+        keep1[step, na:mid] = a_parts[3]
+        keep1[step, mid:mid + nb] = b_parts[2]
+        keep1[step, mid + nb:2 * nab] = b_parts[3]
 
     def second(step):
         stage1[step, "a"].wait_recv()
-        ay_send[step] = (keep1[step, 0:unit] + ax_recv[step, 0:unit].astype(f32)).astype(bf16)
-        stage2[step, "a"] = send(ay_send.at[step], ay_recv.at[step], ydev)
-        keep2[step, 0:unit] = keep1[step, unit:u2] + ax_recv[step, unit:u2].astype(f32)
+        ay_send[step] = (keep1[step, 0:na] + ax_recv[step, 0:na].astype(f32)).astype(bf16)
+        stage2[step, "a"] = send(ay_send.at[step], ay_recv.at[step], b_dev[step % 2])
         stage1[step, "b"].wait_recv()
-        bx_send[step] = (keep1[step, u2:u2 + unit] + by_recv[step, 0:unit].astype(f32)).astype(bf16)
-        stage2[step, "b"] = send(bx_send.at[step], bx_recv.at[step], xdev)
-        keep2[step, unit:u2] = keep1[step, u2 + unit:u4] + by_recv[step, unit:u2].astype(f32)
+        mid = 2 * na
+        bx_send[step] = (keep1[step, mid:mid + nb] + by_recv[step, 0:nb].astype(f32)).astype(bf16)
+        stage2[step, "b"] = send(bx_send.at[step], bx_recv.at[step], a_dev[step % 2])
+        keep2[step, 0:na] = keep1[step, na:mid] + ax_recv[step, na:mid].astype(f32)
+        keep2[step, na:nab] = keep1[step, mid + nb:2 * nab] + by_recv[step, nb:2 * nb].astype(f32)
 
     def third_sum(step, lo, hi):
         got = ay_recv if lo == 0 else bx_recv
         return keep2[step, lo:hi] + got[step].astype(f32)
 
+    halves = ((0, na), (na, nab))
+
     def third(step):
         stage2[step, "a"].wait_recv()
         stage2[step, "b"].wait_recv()
-        halves = ((0, unit), (unit, u2))
         if step in (0, 2):
             for lo, hi in halves:
                 pz_send[step // 2, lo:hi] = third_sum(step, lo, hi).astype(bf16)
@@ -277,8 +300,8 @@
                 pw_send[lo:hi] = (third_sum(step, lo, hi) + pz_recv[0, lo:hi].astype(f32)).astype(bf16)
             zcopy["p", 1] = send(pw_send, pw_recv, z1dev)
         else:
+            zcopy["p", 1].wait_recv()
             zcopy["p", 2].wait_recv()
-            zcopy["p", 1].wait_recv()
             for lo, hi in halves:
                 out[lo:hi] = third_sum(step, lo, hi) + pz_recv[1, lo:hi].astype(f32) + pw_recv[lo:hi].astype(f32)
 
@@ -286,6 +309,22 @@
         zcopy["c", 0].wait_recv()
         cw_send[...] = (ck[0] + cz_recv[0].astype(f32)).astype(bf16)
         zcopy["c", 1] = send(cw_send, cw_recv, z1dev)
+
+    def c_sum(lo, hi):
+        return ck[1, lo:hi] + cz_recv[1, lo:hi].astype(f32) + cw_recv[lo:hi].astype(f32)
+
+    def c_x():
+        zcopy["c", 2].wait_recv()
+        zcopy["c", 1].wait_recv()
+        cx_send[...] = c_sum(0, 2 * nc).astype(bf16)
+        zcopy["cx"] = send(cx_send, cx_recv, xdev)
+        ckx[...] = c_sum(2 * nc, 4 * nc)
+
+    def c_y():
+        zcopy["cx"].wait_recv()
+        cy_send[...] = (ckx[0:nc] + cx_recv[0:nc].astype(f32)).astype(bf16)
+        zcopy["cy"] = send(cy_send, cy_recv, ydev)
+        ckx[nc:2 * nc] = ckx[nc:2 * nc] + cx_recv[nc:2 * nc].astype(f32)
 
     build(0)
     for step in range(4):
@@ -294,40 +333,29 @@
             pl.semaphore_wait(barrier, 5)
         stage1[step, "c"] = send(c_send.at[step], c_recv.at[step], core)
         product(step, 1, own, f32)
+        if step == 2:
+            c_across()
         if step < 3:
             build(step + 1)
         first(step)
-        if step >= 1:
-            second(step - 1)
-        if step == 1:
-            c_across()
         if step >= 2:
-            third(step - 2)
-
+            second(step - 2)
+    third(0)
+    second(2)
+    c_x()
     second(3)
+    third(1)
+    c_y()
     third(2)
-    zcopy["c", 2].wait_recv()
-    zcopy["c", 1].wait_recv()
-
-    def c_sum(lo, hi):
-        return ck[1, lo:hi] + cz_recv[1, lo:hi].astype(f32) + cw_recv[lo:hi].astype(f32)
-
-    cx_send[...] = c_sum(0, u2).astype(bf16)
-    cx = send(cx_send, cx_recv, xdev)
-    ckx[...] = c_sum(u2, u4)
     third(3)
-    cx.wait_recv()
-    cy_send[...] = (ckx[0:unit] + cx_recv[0:unit].astype(f32)).astype(bf16)
-    cy = send(cy_send, cy_recv, ydev)
-    ckx[unit:u2] = ckx[unit:u2] + cx_recv[unit:u2].astype(f32)
-    cy.wait_recv()
-    out[u2:3 * unit] = ckx[unit:u2] + cy_recv[...].astype(f32)
+    zcopy["cy"].wait_recv()
+    out[nab:shard] = ckx[nc:2 * nc] + cy_recv[...].astype(f32)
     aux_lanes = gamma.shape[1]
-    gamma[...] = out[0:3 * unit, 0:aux_lanes] * scale
-    out[3 * unit:] = jnp.zeros((out.shape[0] - 3 * unit, lanes), f32)
+    gamma[...] = out[0:shard, 0:aux_lanes] * scale
+    out[shard:] = jnp.zeros((out.shape[0] - shard, lanes), f32)
     turned[...] = out[:, aux_lanes:].T * scale
     strip = virt.shape[0]
-    virt[...] = turned[pl.ds(pl.multiple_of(z0 * (turned.shape[0] - strip), 8), strip), 0:3 * unit]
+    virt[...] = turned[pl.ds(pl.multiple_of(z0 * (turned.shape[0] - strip), 8), strip), 0:shard]
     for copy in started:
         copy.wait_send()
 
@@ -342,7 +370,8 @@
     block = rows // pao_blocks.shape[1]
     ao_count = NBLK * block
     shard = ao_count // n_pair
-    unit = shard // 3
+    na, nb, nc = group_rows(shard)
+    nab = na + nb
     aux_lanes = ABPO * block
     lanes = aux_lanes + 2 * block
     width = pairs * rank
@@ -356,7 +385,6 @@
     def full(*dims):
         return pltpu.VMEM(dims + (lanes,), jnp.float32)
 
-    u1, u2, u4 = unit, 2 * unit, 4 * unit
     gamma, virt = pl.pallas_call(
         functools.partial(kernel, scale),
         out_shape=[
@@ -371,16 +399,16 @@
             pltpu.VMEM((width, rows), jnp.bfloat16),
             pltpu.VMEM((width, rows), jnp.bfloat16),
             pltpu.VMEM((2, SUB, width), jnp.int32),
-            pltpu.VMEM((24 * unit, width), jnp.bfloat16),
+            pltpu.VMEM((8 * shard, width), jnp.bfloat16),
             pltpu.VMEM((2, width, lanes), jnp.bfloat16),
-            full(12 * unit),
-            half(4, 12 * unit), half(4, 12 * unit),
-            half(4, u2), half(4, u2), half(4, u1), half(4, u1),
-            half(4, u2), half(4, u2), half(4, u1), half(4, u1),
-            full(4, u4), full(4, u2),
-            half(2, u4), half(2, u4), half(u4), half(u4), full(2, u4),
-            half(2, u2), half(2, u2), half(u2), half(u2),
-            half(u2), half(u2), half(u1), half(u1), full(u2),
+            full(4 * shard),
+            half(4, 4 * shard), half(4, 4 * shard),
+            half(4, 2 * na), half(4, 2 * na), half(4, na), half(4, na),
+            half(4, 2 * nb), half(4, 2 * nb), half(4, nb), half(4, nb),
+            full(4, 2 * nab), full(4, nab),
+            half(2, 4 * nc), half(2, 4 * nc), half(4 * nc), half(4 * nc), full(2, 4 * nc),
+            half(2, nab), half(2, nab), half(nab), half(nab),
+            half(2 * nc), half(2 * nc), half(nc), half(nc), full(2 * nc),
             pltpu.VMEM((2 * block, TILE), jnp.float32),
             pltpu.SemaphoreType.DMA((COPIES,)),
             pltpu.SemaphoreType.DMA((COPIES,)),

time: 45.6 us -> 39.3 us (0.86)
  Pallas kernels: 42.5 us -> 36.2 us
    pallas_call x1, Pallas kernels: 42.5 us -> 36.2 us  [by_kernel(): pl.pallas_call(functools.partial(kernel, scale), out_shape=[jax.ShapeDtyp...]
where the time goes in v3:
time: 39.3 us; the launch traced here: 39.1 us
  Pallas kernels  36.2 us (92%)
  local copies, waits for them, and re-layouts  2.29 us (6%)
  between operations  0.65 us (2%)
    pallas_call x1, Pallas kernels, by_kernel(): pl.pallas_call(functools.partial(kernel, scale), out_shape=[jax.ShapeDtyp...  36.2 us
    unnamed x4, local copies, waits for them, and re-layouts  2.29 us

profile of v3, /device:TPU:0, one launch (start us, length us, event | category | flops | bytes accessed | tf_op | source)
XLA Modules:
  0.0 39.1 jit_solution(7375388818288062781)
XLA Ops:
  0.6 36.2 %shard_map.86 = (f32[96,512]{1,0:T(8,128)}, f32[192,96]{1,0:T(8,128)}) custom-call(bf16[16,64,256]{2,1,0:T(8,128)(2,1)} %bitcast.6, bf16[16,64,64]{2,1,0:T(8,128)(2,1)} %amps.1, bf16[16,64,64]{2,1,0:T(8,128)(2,1)} %dens.1, bf16[16,64,256]{2,1,0:T(8,128)(2,1)} %bitcast.7, s32[2,16]{1,0:T(2,128)} %bitcast.9, s32[2,16]{1,0:T(2,128)} %bitcast.10, s32[2,16]{1,0:T(2,128)} %bitcast.11), custom_call_target="tpu_custom_call" | custom-call | tf_op jit(solution)/shard_map/pallas_call | solution.py:388
  36.8 0.0 copy-start
  36.8 1.6 %copy.11 = f32[512,96]{0,1:T(8,128)} copy(f32[512,96]{0,1:T(8,128)} %bitcast.8) | data formatting | bytes 393216
  38.5 0.0 copy-done
  38.5 0.6 %copy.12 = f32[192,96]{1,0:T(8,128)} copy(f32[192,96]{1,0:T(8,128)S(1)} %copy-done) | data formatting | bytes 147456
Async XLA Ops:
  36.8 1.7 %copy-start = (f32[192,96]{1,0:T(8,128)S(1)}, f32[192,96]{1,0:T(8,128)}, u32[]{:S(2)}) copy-start(f32[192,96]{1,0:T(8,128)} %get-tuple-element.9) | copy-start | bytes 221188
